TPU v7x, 128 devices: a whole 4x4x4 slice. The times are simulated.
128 devices in a mesh: sub: 16 (over x_hi, z, core), sta: 8 (over x_lo, y).
Axes of the slice: x: 4 (x_hi: 2, x_lo: 2; x = x_hi * 2 + x_lo), y: 4, z: 4, core: 2. Of those that a mesh axis runs over, the one named last changes fastest.
Arguments:
- voltages: bfloat16 [16, 2, 64, 65536], P('sub', None, 'sta'), may hold values from -6 to 6
- beam_weights: bfloat16 [16, 2, 32, 64], P('sub'), may hold values from -0.5 to 0.5
- station_delays: int32 [64], P('sta'), may hold values from 0 to 16383
- dm_index: int32 [32, 1], P('sta'), may hold values from 1 to 8
Outputs:
- dedispersed: float32 [16, 2, 32, 1, 65536], P(None, None, None, None, ('sub', 'sta'))
- intensity: float32 [32, 1, 65536], P(None, None, ('sub', 'sta'))
Inputs may be any that keep to these rules, and one draw needn't show every extreme that they name: `station_delays`: delays in whole samples. `dm_index`: dispersion measure in steps of 10.
All inputs are finite; a program needn't handle non-finite values.
Results may differ from a plain program's by a relative error of at most 0.0006.
Values may be sent and summed in bfloat16 or wider, within the bound.
A program may use at most 320 MiB of HBM per device.

v0:
```python
import jax
import jax.numpy as jnp
from jax import lax
from jax.sharding import PartitionSpec as P

ROOT = 256
TWO_PI = 6.283185307179586
DISPERSION = 4148808000.0
DM_STEP = 10.0
BASE_FREQ = 120.0
CHANNEL_WIDTH = 0.1953125
HIGHEST = lax.Precision.HIGHEST


def in_blocks(array, dim, devices):
    shape = array.shape
    tiles = array.reshape(*shape[:dim], devices, shape[dim] // devices, *shape[dim + 1 :])
    return jnp.moveaxis(tiles, dim, 0)


def in_order(tiles, dim):
    shape = list(tiles.shape[1:])
    shape[dim] *= tiles.shape[0]
    return jnp.moveaxis(tiles, 0, dim).reshape(shape)


def joined_exchange(array, axis, axes, splits, concats):
    sizes = [lax.axis_size(a) for a in axes]
    tiles = in_blocks(array, splits[0], sizes[0])
    tiles = jnp.moveaxis(in_blocks(tiles, splits[1] + 1, sizes[1]), 0, 1)
    inside = tiles.shape[2:]
    tiles = tiles.reshape(-1, *inside)
    tiles = lax.all_to_all(tiles, axis, split_axis=0, concat_axis=0, tiled=True)
    tiles = in_order(tiles.reshape(*sizes, *inside), concats[0] + 1)
    return in_order(tiles, concats[1])


def angle_tables(rows_len, modulus):
    first = jnp.arange(rows_len, dtype=jnp.int32)[:, None]
    second = jnp.arange(rows_len, dtype=jnp.int32)[None, :]
    product = first * second % modulus
    angles = TWO_PI * product.astype(jnp.float32) / modulus
    return (jnp.cos(angles), jnp.sin(angles))


def chirp_base(subband, root_len, total_len):
    first = jnp.arange(root_len, dtype=jnp.int32)[:, None]
    second = jnp.arange(root_len, dtype=jnp.int32)[None, :]
    positions = first + root_len * second
    signed_bin = jnp.where(positions < total_len // 2, positions, positions - total_len)
    offset = (CHANNEL_WIDTH * signed_bin.astype(jnp.float32) / total_len)[None]
    centre = (BASE_FREQ + CHANNEL_WIDTH * (subband.astype(jnp.float32) + 0.5))[:, None, None]
    return TWO_PI * DISPERSION * offset * offset / (centre * centre * (centre + offset))


def left_dft(cos_table, sin_table, x_real, x_imag, flip_sign):
    real_part = jnp.einsum(
        "kt,...tu->...ku", cos_table, x_real, precision=HIGHEST
    ) + flip_sign * jnp.einsum("kt,...tu->...ku", sin_table, x_imag, precision=HIGHEST)
    imag_part = jnp.einsum(
        "kt,...tu->...ku", cos_table, x_imag, precision=HIGHEST
    ) - flip_sign * jnp.einsum("kt,...tu->...ku", sin_table, x_real, precision=HIGHEST)
    return (real_part, imag_part)


def right_dft(cos_table, sin_table, x_real, x_imag, flip_sign):
    real_part = jnp.einsum(
        "...kt,tm->...km", x_real, cos_table, precision=HIGHEST
    ) + flip_sign * jnp.einsum("...kt,tm->...km", x_imag, sin_table, precision=HIGHEST)
    imag_part = jnp.einsum(
        "...kt,tm->...km", x_imag, cos_table, precision=HIGHEST
    ) - flip_sign * jnp.einsum("...kt,tm->...km", x_real, sin_table, precision=HIGHEST)
    return (real_part, imag_part)


def beam_terms(w_block, v_real, v_imag):
    w_real = w_block[:, 0]
    w_imag = w_block[:, 1]
    real_part = jnp.einsum(
        "sbk,skt->bst", w_real, v_real, preferred_element_type=jnp.float32
    ) - jnp.einsum("sbk,skt->bst", w_imag, v_imag, preferred_element_type=jnp.float32)
    imag_part = jnp.einsum(
        "sbk,skt->bst", w_real, v_imag, preferred_element_type=jnp.float32
    ) + jnp.einsum("sbk,skt->bst", w_imag, v_real, preferred_element_type=jnp.float32)
    return jnp.stack([real_part, imag_part], axis=2)


def shards(voltages, beam_weights, station_delays, dm_index):
    sub_dev = voltages.shape[0]
    total_len = voltages.shape[3]
    local_beams = dm_index.shape[0]
    trials = dm_index.shape[1]
    root_len = ROOT
    doubled = jnp.concatenate([voltages, voltages], axis=3)
    shifted = jax.vmap(
        lambda rows, shift_by: lax.dynamic_slice_in_dim(rows, total_len - shift_by, total_len, 2),
        in_axes=(2, 0),
        out_axes=2,
    )(doubled, station_delays)
    own_weights = lax.dynamic_slice_in_dim(
        beam_weights, lax.axis_index("sta") * local_beams, local_beams, 2
    )
    shard_piece = lax.all_gather(shifted, "sta", axis=2, tiled=True)
    beams = beam_terms(own_weights, shard_piece[:, 0], shard_piece[:, 1])
    cos_root, sin_root = angle_tables(root_len, root_len)
    cos_twist, sin_twist = angle_tables(root_len, total_len)
    x_real = beams[:, :, 0].reshape(local_beams, sub_dev, root_len, root_len)
    x_imag = beams[:, :, 1].reshape(local_beams, sub_dev, root_len, root_len)
    a_real, a_imag = left_dft(cos_root, sin_root, x_real, x_imag, 1.0)
    b_real = a_real * cos_twist + a_imag * sin_twist
    b_imag = a_imag * cos_twist - a_real * sin_twist
    s_real, s_imag = right_dft(cos_root, sin_root, b_real, b_imag, 1.0)
    subband = lax.axis_index("sub") * sub_dev + jnp.arange(sub_dev, dtype=jnp.int32)
    base_phase = chirp_base(subband, root_len, total_len)
    dm_value = DM_STEP * dm_index.astype(jnp.float32)
    phase_table = dm_value[:, None, :, None, None] * base_phase[None, :, None, :, :]
    h_real = jnp.cos(phase_table)
    h_imag = jnp.sin(phase_table)
    c_real = s_real[:, :, None] * h_real - s_imag[:, :, None] * h_imag
    c_imag = s_real[:, :, None] * h_imag + s_imag[:, :, None] * h_real
    d_real, d_imag = right_dft(cos_root, sin_root, c_real, c_imag, -1.0)
    e_real = d_real * cos_twist - d_imag * sin_twist
    e_imag = d_imag * cos_twist + d_real * sin_twist
    scale = 1.0 / total_len
    out_real = jnp.einsum("tk,bsjku->sbjtu", cos_root, e_real, precision=HIGHEST) - jnp.einsum(
        "tk,bsjku->sbjtu", sin_root, e_imag, precision=HIGHEST
    )
    out_imag = jnp.einsum("tk,bsjku->sbjtu", cos_root, e_imag, precision=HIGHEST) + jnp.einsum(
        "tk,bsjku->sbjtu", sin_root, e_real, precision=HIGHEST
    )
    series = jnp.stack([out_real * scale, out_imag * scale], axis=1).reshape(
        sub_dev, 2, local_beams, trials, total_len
    )
    moved = joined_exchange(series, ("sub", "sta"), ("sub", "sta"), (4, 4), (0, 2))
    intensity = jnp.mean(moved[:, 0] * moved[:, 0] + moved[:, 1] * moved[:, 1], axis=0)
    return (moved, intensity)


def solution(mesh):
    return jax.shard_map(
        shards,
        mesh=mesh,
        in_specs=(
            P("sub", None, "sta", None),
            P("sub", None, None, None),
            P("sta"),
            P("sta", None),
        ),
        out_specs=(P(None, None, None, None, ("sub", "sta")), P(None, None, ("sub", "sta"))),
        check_vma=False,
    )
```

profile of v0, /device:TPU:0, one launch (start us, length us, event | category | flops | bytes accessed | tf_op | source)
XLA Modules:
  0.0 361.2 jit_solution(14308672278880408520)
XLA Ops:
  7.2 3.8 %copy.62 = bf16[1,2,8,65536]{3,1,0,2:T(2,128)(2,1)S(1)} copy(bf16[1,2,8,65536]{3,2,1,0:T(8,128)(2,1)} %param.4) | data formatting | bytes 4194304 | tf_op args[0]
  11.0 6.1 %maximum_bitcast_fusion = bf16[8,1,2,131072]{3,2,1,0:T(2,128)(2,1)} fusion(bf16[1,2,8,65536]{3,1,0,2:T(2,128)(2,1)S(1)} %copy.62), kind=kLoop, calls=%fused_computation.8 | loop fusion | flops 8388608 | bytes 6291456 | tf_op jit(solution)/shard_map/vmap()/transpose | solution.py:96
  17.1 31.7 %while.1 = (s32[]{:T(128)}, bf16[8,1,2,131072]{3,2,1,0:T(2,128)(2,1)}, s32[8,4]{0,1:T(4,128)S(1)}, bf16[8,1,2,65536]{3,2,1,0:T(2,128)(2,1)}, s32[]{:T(128)}) while((s32[]{:T(128)}, bf16[8,1,2,131072]{3,2,1,0:T(2,128)(2,1)}, s32[8,4]{0,1:T(4,128)S(1)}, bf16[8,1,2,65536]{3,2,1,0:T(2,128)(2,1)}, s32[]{:T(128)}) %tuple.26), condition=%wide.while_cond, body=%wide.while_body.sunk | while | flops 2 | bytes 525937 | solution.py:96
  17.8 3.2 dynamic-slice_dynamic-update-slice_fusion.2
  21.7 3.2 dynamic-slice_dynamic-update-slice_fusion.2
  25.6 3.2 dynamic-slice_dynamic-update-slice_fusion.2
  29.5 3.2 dynamic-slice_dynamic-update-slice_fusion.2
  33.3 3.2 dynamic-slice_dynamic-update-slice_fusion.2
  37.2 3.2 dynamic-slice_dynamic-update-slice_fusion.2
  41.1 3.2 dynamic-slice_dynamic-update-slice_fusion.2
  45.0 3.2 dynamic-slice_dynamic-update-slice_fusion.2
  48.8 4.1 %copy.119 = bf16[8,1,2,65536]{3,0,2,1:T(8,128)(2,1)} copy(bf16[8,1,2,65536]{3,2,1,0:T(2,128)(2,1)} %get-tuple-element.9) | data formatting | bytes 4194304 | tf_op jit(solution)/shard_map/vmap()/gather | solution.py:96
  54.4 171.7 %all-gather.2.cloned.1.call-done = bf16[1,2,64,65536]{3,2,1,0:T(8,128)(2,1)} async-done(((bf16[1,2,8,65536]{3,2,1,0:T(8,128)(2,1)}), bf16[1,2,64,65536]{3,2,1,0:T(8,128)(2,1)}) %all-gather.2.cloned.1.call-update) | async-done | bytes 16777232 | tf_op jit(solution)/shard_map/all_gather | solution.py:103
  226.0 4.7 %fusion.1 = f32[65536,4]{0,1:T(4,128)S(1)} fusion(bf16[1,2,64,65536]{3,2,1,0:T(8,128)(2,1)} %all-gather.2.cloned.1.call-done, bf16[1,2,32,64]{3,2,1,0:T(8,128)(2,1)S(1)} %copy-done, s32[]{:T(128)S(6)} %select_n.87), kind=kOutput, calls=%fused_computation.7 | convolution fusion | flops 33554432 | bytes 9438212 | tf_op jit(solution)/shard_map/sbk,skt->bst/dot_general | solution.py:82
  230.8 5.3 %convolution_add_fusion = f32[65536,4]{0,1:T(4,128)S(1)} fusion(f32[65536,4]{0,1:T(4,128)S(1)} %fusion.1, bf16[1,2,64,65536]{3,2,1,0:T(8,128)(2,1)} %all-gather.2.cloned.1.call-done, bf16[1,2,32,64]{3,2,1,0:T(8,128)(2,1)S(1)} %copy-done, s32[]{:T(128)S(6)} %add.214, s32[]{:T(128)S(6)} %select_n.87), kind=kOutput, calls=%fused_computation.2 | convolution fusion | flops 33816576 | bytes 10486792 | tf_op jit(solution)/shard_map/sbk,skt->bst/dot_general | solution.py:84
  260.9 5.6 %fusion.51 = f32[4,256,256]{2,1,0:T(8,128)S(1)} fusion(f32[4,256,256]{2,1,0:T(8,128)S(1)} %convolution_add_fusion.2, f32[4,256,256]{2,1,0:T(8,128)S(1)} %convolution_subtract_fusion.2, f32[256,256]{1,0:T(8,128)S(1)} %multiply_divide_fusion, f32[4]{0:T(128)S(1)} %multiply_bitcast_fusion), kind=kOutput, calls=%fused_computation.83 | convolution fusion | flops 807272448 | bytes 3407888 | tf_op jit(solution)/shard_map/...kt,tm->...km/dot_general | solution.py:70
  266.5 6.0 %fusion.53 = f32[4,256,256]{2,1,0:T(8,128)S(1)} fusion(f32[4,256,256]{2,1,0:T(8,128)S(1)} %convolution_subtract_fusion.2, f32[4,256,256]{2,1,0:T(8,128)S(1)} %convolution_add_fusion.2, f32[256,256]{1,0:T(8,128)S(1)} %multiply_divide_fusion, f32[4]{0:T(128)S(1)} %multiply_bitcast_fusion), kind=kOutput, calls=%fused_computation.85 | convolution fusion | flops 807272448 | bytes 3407888 | tf_op jit(solution)/shard_map/...kt,tm->...km/dot_general | solution.py:67
  272.5 5.6 %fusion.10 = f32[4,256,256]{2,1,0:T(8,128)S(1)} fusion(f32[4,256,256]{2,1,0:T(8,128)S(1)} %fusion.51, f32[4,256,256]{2,1,0:T(8,128)S(1)} %convolution_subtract_fusion.2, f32[4,256,256]{2,1,0:T(8,128)S(1)} %convolution_add_fusion.2, f32[256,256]{1,0:T(8,128)S(1)} %multiply_divide_fusion, f32[4]{0:T(128)S(1)} %multiply_bitcast_fusion), kind=kOutput, calls=%fused_computation.25 | convolution fusion | flops 807796736 | bytes 4456464 | tf_op jit(solution)/shard_map/...kt,tm->...km/dot_general | solution.py:72
  278.2 5.8 %fusion.11 = f32[4,256,256]{2,1,0:T(8,128)S(1)} fusion(f32[4,256,256]{2,1,0:T(8,128)S(1)} %fusion.53, f32[4,256,256]{2,1,0:T(8,128)S(1)} %convolution_add_fusion.2, f32[4,256,256]{2,1,0:T(8,128)S(1)} %convolution_subtract_fusion.2, f32[256,256]{1,0:T(8,128)S(1)} %multiply_divide_fusion, f32[4]{0:T(128)S(1)} %multiply_bitcast_fusion), kind=kOutput, calls=%fused_computation.27 | convolution fusion | flops 807796736 | bytes 4456464 | tf_op jit(solution)/shard_map/...kt,tm->...km/dot_general | solution.py:69
  286.8 3.7 %fusion.47 = f32[4,256,256]{2,1,0:T(8,128)} fusion(f32[4,256,256]{2,1,0:T(8,128)S(1)} %fusion.11, f32[4,256,256]{2,1,0:T(8,128)S(1)} %fusion.10, f32[256,256]{1,0:T(8,128)S(1)} %get-tuple-element.24, f32[256,256]{1,0:T(8,128)S(1)} %get-tuple-element.25), kind=kOutput, calls=%fused_computation.79 | convolution fusion | flops 807010304 | bytes 3670016 | tf_op jit(solution)/shard_map/tk,bsjku->sbjtu/dot_general | solution.py:128
  290.5 4.0 %fusion.9 = f32[1,4,1,256,256]{3,4,1,2,0:T(8,128)} fusion(f32[4,256,256]{2,1,0:T(8,128)S(1)} %fusion.49, f32[4,256,256]{2,1,0:T(8,128)S(1)} %fusion.11, f32[4,256,256]{2,1,0:T(8,128)S(1)} %fusion.10, f32[256,256]{1,0:T(8,128)S(1)} %get-tuple-element.24, f32[256,256]{1,0:T(8,128)S(1)} %get-tuple-element.25), kind=kOutput, calls=%fused_computation.23 | convolution fusion | flops 807534592 | bytes 4718592 | tf_op jit(solution)/shard_map/tk,bsjku->sbjtu/dot_general | solution.py:125
  299.4 4.9 %fusion.7 = f32[1,4,1,256,256]{3,4,1,2,0:T(8,128)} fusion(f32[4,256,256]{2,1,0:T(8,128)} %fusion.47, f32[4,256,256]{2,1,0:T(8,128)S(1)} %fusion.10, f32[4,256,256]{2,1,0:T(8,128)S(1)} %fusion.11, f32[256,256]{1,0:T(8,128)S(1)} %get-tuple-element.24, f32[256,256]{1,0:T(8,128)S(1)} %get-tuple-element.25), kind=kOutput, calls=%fused_computation.20 | convolution fusion | flops 807534592 | bytes 4718592 | tf_op jit(solution)/shard_map/tk,bsjku->sbjtu/dot_general | solution.py:128
  309.4 37.7 %all_to_all.5 = f32[128,1,2,4,1,512]{5,3,2,4,1,0:T(4,128)S(1)} all-to-all(f32[128,1,2,4,1,512]{5,3,2,4,1,0:T(4,128)S(1)} %bitcast.151), channel_id=1, replica_groups=mesh['sub'=16,'sta'=8] {'sub','sta'}, dimensions={0} | all-to-all | bytes 4194304 | tf_op jit(solution)/shard_map/all_to_all | solution.py:33
  349.5 3.5 copy.84
  (63 shorter events, 47.6 us)
Async XLA Ops:
  7.2 218.9 %copy-start = (bf16[1,2,32,64]{3,2,1,0:T(8,128)(2,1)S(1)}, bf16[1,2,32,64]{3,2,1,0:T(8,128)(2,1)}, u32[]{:S(2)}) copy-start(bf16[1,2,32,64]{3,2,1,0:T(8,128)(2,1)} %param.5) | copy-start | bytes 24580
  7.2 218.9 %all-gather.2.cloned.1.call-start = ((), (), s32[]{:S(2)}) async-start(), calls=%async_computation.1 | async-start | bytes 18874368 | tf_op jit(solution)/shard_map/all_gather | solution.py:103
  11.0 6.1 %copy-start.4 = (s32[8]{0:T(128)S(1)}, s32[8]{0:T(128)}, u32[]{:S(2)}) copy-start(s32[8]{0:T(128)} %param.6) | copy-start | bytes 100
  48.8 5.5 %copy-start.5 = (s32[4,1]{0,1:T(1,128)S(1)}, s32[4,1]{0,1:T(1,128)}, u32[]{:S(2)}) copy-start(s32[4,1]{0,1:T(1,128)} %param.7) | copy-start | bytes 52
  226.0 12.8 %copy-start.2 = (bf16[1,2,64,65536]{3,2,1,0:T(8,128)(2,1)S(1)}, bf16[1,2,64,65536]{3,2,1,0:T(8,128)(2,1)}, u32[]{:S(2)}) copy-start(bf16[1,2,64,65536]{3,2,1,0:T(8,128)(2,1)} %all-gather.2.cloned.1.call-done) | copy-start | bytes 50331652
  304.3 1.9 copy-start.3
  348.3 5.8 %copy-start.1 = (bf16[1,2,32,64]{3,2,1,0:T(8,128)(2,1)S(1)}, bf16[1,2,32,64]{3,2,1,0:T(8,128)(2,1)}, u32[]{:S(2)}) copy-start(bf16[1,2,32,64]{3,2,1,0:T(8,128)(2,1)} %param.5) | copy-start | bytes 24580
Sparse Core Ops, SparseCore 0:
  53.0 172.9 all-gather.1
where the time goes:
time: 367 us; the launch traced here: 361 us
  waiting for transfers between devices  172 us (47%)
  matrix products  73.2 us (20%)
  local copies, waits for them, and re-layouts  55.7 us (15%)
  blocking collectives  37.7 us (10%)
  between operations  14.6 us (4%)
  other arithmetic  7.77 us (2%)
    all_gather x1, waiting for transfers between devices, shards(): shard_piece = lax.all_gather(shifted, 'sta', axis=2, tiled=True)  172 us
    all_to_all x1, blocking collectives, joined_exchange(): tiles = lax.all_to_all(tiles, axis, split_axis=0, concat_axis=0, tiled=True)  37.7 us
    gather x24, local copies, waits for them, and re-layouts  31.1 us
    unnamed x16, local copies, waits for them, and re-layouts  8.91 us
    dot_general x2, matrix products, right_dft(): jnp.einsum('...kt,tm->...km', x_imag, sin_table, precision=HIGHEST)  8.8 us
    dot_general x2, matrix products, right_dft(): jnp.einsum('...kt,tm->...km', x_real, cos_table, precision=HIGHEST)  8.8 us
    dot_general x2, matrix products, right_dft(): jnp.einsum('...kt,tm->...km', x_real, sin_table, precision=HIGHEST)  8.4 us
    dot_general x2, matrix products, right_dft(): jnp.einsum('...kt,tm->...km', x_imag, cos_table, precision=HIGHEST)  8.39 us
  transfers between devices with their start and end apart: 1, of which 1 were waited for; matrix products, arithmetic and copies ran while one was open for 0% of the time, Pallas kernels for 0%

commit v1 on v0

--- a/solution.py
+++ b/solution.py
@@ -100,7 +100,7 @@
     own_weights = lax.dynamic_slice_in_dim(
         beam_weights, lax.axis_index("sta") * local_beams, local_beams, 2
     )
-    shard_piece = lax.all_gather(shifted, "sta", axis=2, tiled=True)
+    shard_piece = jnp.concatenate(lax.all_gather(shifted, "sta"), axis=2)
     beams = beam_terms(own_weights, shard_piece[:, 0], shard_piece[:, 1])
     cos_root, sin_root = angle_tables(root_len, root_len)
     cos_twist, sin_twist = angle_tables(root_len, total_len)

time: 367 us -> 367 us (level)
    dot_general x1, matrix products: 1.2 us -> 5.32 us  [beam_terms(): jnp.einsum('sbk,skt->bst', w_real, v_real, preferred_element_type=jnp.flo...]
    dot_general x1, matrix products: 5.33 us -> 1.2 us  [beam_terms(): jnp.einsum('sbk,skt->bst', w_imag, v_real, preferred_element_type=jnp.flo...]
where the time goes in v1:
time: 367 us; the launch traced here: 362 us
  waiting for transfers between devices  172 us (47%)
  matrix products  73.2 us (20%)
  local copies, waits for them, and re-layouts  56.2 us (15%)
  blocking collectives  37.7 us (10%)
  between operations  14.6 us (4%)
  other arithmetic  7.77 us (2%)
    all_gather x1, waiting for transfers between devices, shards(): shard_piece = jnp.concatenate(lax.all_gather(shifted, 'sta'), axis=2)  172 us
    all_to_all x1, blocking collectives, joined_exchange(): tiles = lax.all_to_all(tiles, axis, split_axis=0, concat_axis=0, tiled=True)  37.7 us
    gather x24, local copies, waits for them, and re-layouts  31.1 us
    unnamed x16, local copies, waits for them, and re-layouts  9.39 us
    dot_general x2, matrix products, right_dft(): jnp.einsum('...kt,tm->...km', x_imag, sin_table, precision=HIGHEST)  8.81 us
    dot_general x2, matrix products, right_dft(): jnp.einsum('...kt,tm->...km', x_real, cos_table, precision=HIGHEST)  8.8 us
    dot_general x2, matrix products, right_dft(): jnp.einsum('...kt,tm->...km', x_real, sin_table, precision=HIGHEST)  8.4 us
    dot_general x2, matrix products, right_dft(): jnp.einsum('...kt,tm->...km', x_imag, cos_table, precision=HIGHEST)  8.39 us
  transfers between devices with their start and end apart: 1, of which 1 were waited for; matrix products, arithmetic and copies ran while one was open for 0% of the time, Pallas kernels for 0%

profile of v1, /device:TPU:0, one launch (start us, length us, event | category | flops | bytes accessed | tf_op | source)
XLA Modules:
  0.0 361.7 jit_solution(675366072364479937)
XLA Ops:
  7.2 3.8 %copy.62 = bf16[1,2,8,65536]{3,1,0,2:T(2,128)(2,1)S(1)} copy(bf16[1,2,8,65536]{3,2,1,0:T(8,128)(2,1)} %param.4) | data formatting | bytes 4194304 | tf_op args[0]
  11.0 6.1 %maximum_bitcast_fusion = bf16[8,1,2,131072]{3,2,1,0:T(2,128)(2,1)} fusion(bf16[1,2,8,65536]{3,1,0,2:T(2,128)(2,1)S(1)} %copy.62), kind=kLoop, calls=%fused_computation.8 | loop fusion | flops 8388608 | bytes 6291456 | tf_op jit(solution)/shard_map/vmap()/transpose | solution.py:96
  17.1 31.7 %while.1 = (s32[]{:T(128)}, bf16[8,1,2,131072]{3,2,1,0:T(2,128)(2,1)}, s32[8,4]{0,1:T(4,128)S(1)}, bf16[8,1,2,65536]{3,2,1,0:T(2,128)(2,1)}, s32[]{:T(128)}) while((s32[]{:T(128)}, bf16[8,1,2,131072]{3,2,1,0:T(2,128)(2,1)}, s32[8,4]{0,1:T(4,128)S(1)}, bf16[8,1,2,65536]{3,2,1,0:T(2,128)(2,1)}, s32[]{:T(128)}) %tuple.26), condition=%wide.while_cond, body=%wide.while_body.sunk | while | flops 2 | bytes 525937 | solution.py:96
  17.8 3.2 dynamic-slice_dynamic-update-slice_fusion.2
  21.7 3.2 dynamic-slice_dynamic-update-slice_fusion.2
  25.6 3.2 dynamic-slice_dynamic-update-slice_fusion.2
  29.5 3.2 dynamic-slice_dynamic-update-slice_fusion.2
  33.3 3.2 dynamic-slice_dynamic-update-slice_fusion.2
  37.2 3.2 dynamic-slice_dynamic-update-slice_fusion.2
  41.1 3.2 dynamic-slice_dynamic-update-slice_fusion.2
  45.0 3.2 dynamic-slice_dynamic-update-slice_fusion.2
  48.8 4.1 %copy.119 = bf16[8,1,2,65536]{3,0,1,2:T(8,128)(2,1)} copy(bf16[8,1,2,65536]{3,2,1,0:T(2,128)(2,1)} %get-tuple-element.9) | data formatting | bytes 4194304 | tf_op jit(solution)/shard_map/vmap()/gather | solution.py:96
  54.4 171.7 %all-gather.3.cloned.1.call-done = bf16[8,2,8,65536]{3,2,0,1:T(8,128)(2,1)} async-done(((bf16[1,2,8,65536]{3,2,0,1:T(8,128)(2,1)}), bf16[8,2,8,65536]{3,2,0,1:T(8,128)(2,1)}) %all-gather.3.cloned.1.call-update) | async-done | bytes 16777232 | tf_op jit(solution)/shard_map/all_gather | solution.py:103
  226.0 4.7 %fusion.1 = f32[65536,4]{0,1:T(4,128)S(1)} fusion(bf16[1,2,64,65536]{3,2,1,0:T(8,128)(2,1)} %bitcast.147, bf16[1,2,32,64]{3,2,1,0:T(8,128)(2,1)S(1)} %copy-done, s32[]{:T(128)S(6)} %select_n.87), kind=kOutput, calls=%fused_computation.7 | convolution fusion | flops 33554432 | bytes 9438212 | tf_op jit(solution)/shard_map/sbk,skt->bst/dot_general | solution.py:82
  230.8 5.3 %fusion = f32[65536,4]{0,1:T(4,128)S(1)} fusion(bf16[1,2,64,65536]{3,2,1,0:T(8,128)(2,1)} %bitcast.148, bf16[1,2,32,64]{3,2,1,0:T(8,128)(2,1)S(1)} %copy-done, s32[]{:T(128)S(6)} %select_n.87), kind=kOutput, calls=%fused_computation.6 | convolution fusion | flops 33554432 | bytes 9438212 | tf_op jit(solution)/shard_map/sbk,skt->bst/dot_general | solution.py:79
  261.3 5.6 %fusion.51 = f32[4,256,256]{2,1,0:T(8,128)S(1)} fusion(f32[4,256,256]{2,1,0:T(8,128)S(1)} %convolution_add_fusion.2, f32[4,256,256]{2,1,0:T(8,128)S(1)} %convolution_subtract_fusion.2, f32[256,256]{1,0:T(8,128)S(1)} %multiply_divide_fusion, f32[4]{0:T(128)S(1)} %multiply_bitcast_fusion), kind=kOutput, calls=%fused_computation.83 | convolution fusion | flops 807272448 | bytes 3407888 | tf_op jit(solution)/shard_map/...kt,tm->...km/dot_general | solution.py:70
  267.0 6.0 %fusion.53 = f32[4,256,256]{2,1,0:T(8,128)S(1)} fusion(f32[4,256,256]{2,1,0:T(8,128)S(1)} %convolution_subtract_fusion.2, f32[4,256,256]{2,1,0:T(8,128)S(1)} %convolution_add_fusion.2, f32[256,256]{1,0:T(8,128)S(1)} %multiply_divide_fusion, f32[4]{0:T(128)S(1)} %multiply_bitcast_fusion), kind=kOutput, calls=%fused_computation.85 | convolution fusion | flops 807272448 | bytes 3407888 | tf_op jit(solution)/shard_map/...kt,tm->...km/dot_general | solution.py:67
  273.0 5.6 %fusion.10 = f32[4,256,256]{2,1,0:T(8,128)S(1)} fusion(f32[4,256,256]{2,1,0:T(8,128)S(1)} %fusion.51, f32[4,256,256]{2,1,0:T(8,128)S(1)} %convolution_subtract_fusion.2, f32[4,256,256]{2,1,0:T(8,128)S(1)} %convolution_add_fusion.2, f32[256,256]{1,0:T(8,128)S(1)} %multiply_divide_fusion, f32[4]{0:T(128)S(1)} %multiply_bitcast_fusion), kind=kOutput, calls=%fused_computation.25 | convolution fusion | flops 807796736 | bytes 4456464 | tf_op jit(solution)/shard_map/...kt,tm->...km/dot_general | solution.py:72
  278.7 5.8 %fusion.11 = f32[4,256,256]{2,1,0:T(8,128)S(1)} fusion(f32[4,256,256]{2,1,0:T(8,128)S(1)} %fusion.53, f32[4,256,256]{2,1,0:T(8,128)S(1)} %convolution_add_fusion.2, f32[4,256,256]{2,1,0:T(8,128)S(1)} %convolution_subtract_fusion.2, f32[256,256]{1,0:T(8,128)S(1)} %multiply_divide_fusion, f32[4]{0:T(128)S(1)} %multiply_bitcast_fusion), kind=kOutput, calls=%fused_computation.27 | convolution fusion | flops 807796736 | bytes 4456464 | tf_op jit(solution)/shard_map/...kt,tm->...km/dot_general | solution.py:69
  287.3 3.7 %fusion.47 = f32[4,256,256]{2,1,0:T(8,128)} fusion(f32[4,256,256]{2,1,0:T(8,128)S(1)} %fusion.11, f32[4,256,256]{2,1,0:T(8,128)S(1)} %fusion.10, f32[256,256]{1,0:T(8,128)S(1)} %get-tuple-element.24, f32[256,256]{1,0:T(8,128)S(1)} %get-tuple-element.25), kind=kOutput, calls=%fused_computation.79 | convolution fusion | flops 807010304 | bytes 3670016 | tf_op jit(solution)/shard_map/tk,bsjku->sbjtu/dot_general | solution.py:128
  290.9 4.0 %fusion.9 = f32[1,4,1,256,256]{3,4,1,2,0:T(8,128)} fusion(f32[4,256,256]{2,1,0:T(8,128)S(1)} %fusion.49, f32[4,256,256]{2,1,0:T(8,128)S(1)} %fusion.11, f32[4,256,256]{2,1,0:T(8,128)S(1)} %fusion.10, f32[256,256]{1,0:T(8,128)S(1)} %get-tuple-element.24, f32[256,256]{1,0:T(8,128)S(1)} %get-tuple-element.25), kind=kOutput, calls=%fused_computation.23 | convolution fusion | flops 807534592 | bytes 4718592 | tf_op jit(solution)/shard_map/tk,bsjku->sbjtu/dot_general | solution.py:125
  299.9 4.9 %fusion.7 = f32[1,4,1,256,256]{3,4,1,2,0:T(8,128)} fusion(f32[4,256,256]{2,1,0:T(8,128)} %fusion.47, f32[4,256,256]{2,1,0:T(8,128)S(1)} %fusion.10, f32[4,256,256]{2,1,0:T(8,128)S(1)} %fusion.11, f32[256,256]{1,0:T(8,128)S(1)} %get-tuple-element.24, f32[256,256]{1,0:T(8,128)S(1)} %get-tuple-element.25), kind=kOutput, calls=%fused_computation.20 | convolution fusion | flops 807534592 | bytes 4718592 | tf_op jit(solution)/shard_map/tk,bsjku->sbjtu/dot_general | solution.py:128
  309.9 37.7 %all_to_all.5 = f32[128,1,2,4,1,512]{5,3,2,4,1,0:T(4,128)S(1)} all-to-all(f32[128,1,2,4,1,512]{5,3,2,4,1,0:T(4,128)S(1)} %bitcast.160), channel_id=1, replica_groups=mesh['sub'=16,'sta'=8] {'sub','sta'}, dimensions={0} | all-to-all | bytes 4194304 | tf_op jit(solution)/shard_map/all_to_all | solution.py:33
  350.0 3.5 copy.84
  (63 shorter events, 48.1 us)
Async XLA Ops:
  7.2 218.9 %copy-start = (bf16[1,2,32,64]{3,2,1,0:T(8,128)(2,1)S(1)}, bf16[1,2,32,64]{3,2,1,0:T(8,128)(2,1)}, u32[]{:S(2)}) copy-start(bf16[1,2,32,64]{3,2,1,0:T(8,128)(2,1)} %param.5) | copy-start | bytes 24580
  7.2 218.9 %all-gather.3.cloned.1.call-start = ((), (), s32[]{:S(2)}) async-start(), calls=%async_computation.1 | async-start | bytes 18874368 | tf_op jit(solution)/shard_map/all_gather | solution.py:103
  11.0 6.1 %copy-start.4 = (s32[8]{0:T(128)S(1)}, s32[8]{0:T(128)}, u32[]{:S(2)}) copy-start(s32[8]{0:T(128)} %param.6) | copy-start | bytes 100
  48.8 5.5 %copy-start.5 = (s32[4,1]{0,1:T(1,128)S(1)}, s32[4,1]{0,1:T(1,128)}, u32[]{:S(2)}) copy-start(s32[4,1]{0,1:T(1,128)} %param.7) | copy-start | bytes 52
  226.0 10.5 %copy-start.2 = (bf16[8,2,8,65536]{3,2,0,1:T(8,128)(2,1)S(1)}, bf16[8,2,8,65536]{3,2,0,1:T(8,128)(2,1)}, u32[]{:S(2)}) copy-start(bf16[8,2,8,65536]{3,2,0,1:T(8,128)(2,1)} %all-gather.3.cloned.1.call-done) | copy-start | bytes 50331652
  304.8 1.9 copy-start.3
  348.8 5.8 %copy-start.1 = (bf16[1,2,32,64]{3,2,1,0:T(8,128)(2,1)S(1)}, bf16[1,2,32,64]{3,2,1,0:T(8,128)(2,1)}, u32[]{:S(2)}) copy-start(bf16[1,2,32,64]{3,2,1,0:T(8,128)(2,1)} %param.5) | copy-start | bytes 24580
Sparse Core Ops, SparseCore 0:
  53.0 172.9 all-gather.2
